TPU v7x, 32 devices: a whole 2x2x4 slice. The times are simulated.
32 devices in a mesh: row: 4 (over z), col: 8 (over y, x, core).
Axes of the slice: x: 2, y: 2, z: 4, core: 2. Of those that a mesh axis runs over, the one named last changes fastest.
Arguments:
- tokens_in: bfloat16 [8192, 1408], P(('row', 'col')), may hold values from -300 to 300
- ln1_gain: bfloat16 [1408], replicated, may hold values from 0.099609375 to 1.8984375
- ln1_bias: bfloat16 [1408], replicated, may hold values from -3 to 3
- qkv_weight: bfloat16 [1408, 4224], P('row', 'col'), may hold values from -0.8 to 0.8
- qkv_bias: bfloat16 [4224], P('col'), may hold values from -3 to 3
- proj_weight: bfloat16 [1408, 1408], P('col', 'row'), may hold values from -0.15625 to 0.15625
- proj_bias: bfloat16 [1408], replicated, may hold values from -3 to 3
- ln2_gain: bfloat16 [1408], replicated, may hold values from 0.099609375 to 1.8984375
- ln2_bias: bfloat16 [1408], replicated, may hold values from -3 to 3
- fc1_weight: bfloat16 [1408, 6144], P('row', 'col'), may hold values from -0.15625 to 0.15625
- fc1_bias: bfloat16 [6144], P('col'), may hold values from -3 to 3
- fc2_weight: bfloat16 [1408, 6144], P('row', 'col'), may hold values from -0.078125 to 0.078125
- fc2_bias: bfloat16 [1408], replicated, may hold values from -3 to 3
Outputs:
- tokens_out: bfloat16 [8192, 1408], P(('row', 'col'))
All inputs are finite; a program needn't handle non-finite values.
Results may differ from a plain program's by a relative error of at most 0.01.
Values may be sent and summed in bfloat16 or wider, within the bound.
A program may use at most 64 MiB of HBM per device.

v0:
```python
import jax
import jax.numpy as jnp
from jax import lax
from jax.sharding import PartitionSpec as P

HEADS = 16


def norm_local(values, gain, bias):
    mean = jnp.mean(values, axis=-1, keepdims=True)
    centred = values - mean
    var = jnp.mean(centred * centred, axis=-1, keepdims=True)
    return centred * lax.rsqrt(var + 1e-06) * gain.astype(jnp.float32) + bias.astype(jnp.float32)


def attend(qkv, heads):
    length = qkv.shape[0]
    head_size = qkv.shape[1] // (3 * heads)
    parts = qkv.reshape(length, heads, 3, head_size)
    query = parts[:, :, 0]
    keys = parts[:, :, 1]
    values = parts[:, :, 2]
    block = min(512, length)
    blocks = query.reshape(length // block, block, heads, head_size)
    scale = 1.0 / head_size**0.5

    def one_block(qblock):
        scores = (
            jnp.einsum("qhe,khe->hqk", qblock, keys, preferred_element_type=jnp.float32) * scale
        )
        top = jnp.max(scores, axis=-1, keepdims=True)
        expo = jnp.exp(scores - top)
        probs = (expo / jnp.sum(expo, axis=-1, keepdims=True)).astype(jnp.bfloat16)
        mixed = jnp.einsum("hqk,khe->qhe", probs, values, preferred_element_type=jnp.float32)
        return mixed.astype(jnp.bfloat16).reshape(block, heads * head_size)

    return lax.map(one_block, blocks).reshape(length, heads * head_size)


def project_back(left, right):
    return lax.dot_general(
        left, right, (((1,), (1,)), ((), ())), preferred_element_type=jnp.float32
    )


def local(
    tokens_in,
    ln1_gain,
    ln1_bias,
    qkv_weight,
    qkv_bias,
    proj_weight,
    proj_bias,
    ln2_gain,
    ln2_bias,
    fc1_weight,
    fc1_bias,
    fc2_weight,
    fc2_bias,
):
    local_heads = HEADS // lax.axis_size("col")
    own_rows = tokens_in.shape[0]
    inputs = tokens_in.astype(jnp.float32)
    qkv_full = lax.all_gather(qkv_weight, "row", axis=0, tiled=True)
    proj_full = lax.all_gather(proj_weight, "row", axis=1, tiled=True)
    fc1_full = lax.all_gather(fc1_weight, "row", axis=0, tiled=True)
    fc2_full = lax.all_gather(fc2_weight, "row", axis=0, tiled=True)
    qkv_shift = qkv_bias.astype(jnp.float32)
    fc1_shift = fc1_bias.astype(jnp.float32)
    ln1 = norm_local(inputs, ln1_gain, ln1_bias).astype(jnp.bfloat16)
    product = (
        jnp.dot(
            lax.all_gather(ln1, "col", axis=0, tiled=True),
            qkv_full,
            preferred_element_type=jnp.float32,
        )
        + qkv_shift
    )
    qkv = product.astype(jnp.bfloat16)
    attn = attend(qkv, local_heads)
    proj_whole = lax.all_gather(proj_full, "col", axis=0, tiled=True)
    groups = lax.axis_size("col")
    width = proj_whole.shape[0] // groups
    own_heads = lax.all_to_all(attn, "col", split_axis=0, concat_axis=1, tiled=True)
    lefts = own_heads.reshape(own_rows, groups, width)
    rights = proj_whole.reshape(groups, width, proj_whole.shape[1])
    group_parts = jnp.einsum("rgc,gcd->grd", lefts, rights, preferred_element_type=jnp.float32)
    group_parts = lax.optimization_barrier(group_parts.astype(jnp.bfloat16))
    attn_sum = jnp.sum(group_parts.astype(jnp.float32), axis=0)
    resid = inputs + attn_sum + proj_bias.astype(jnp.float32)
    ln2 = norm_local(resid, ln2_gain, ln2_bias).astype(jnp.bfloat16)
    product = (
        jnp.dot(
            lax.all_gather(ln2, "col", axis=0, tiled=True),
            fc1_full,
            preferred_element_type=jnp.float32,
        )
        + fc1_shift
    )
    hidden = jax.nn.gelu(product, approximate=False).astype(jnp.bfloat16)
    mlp_sum = lax.psum_scatter(
        project_back(hidden, fc2_full).astype(jnp.bfloat16), "col", scatter_dimension=0, tiled=True
    ).astype(jnp.float32)
    result = resid + mlp_sum + fc2_bias.astype(jnp.float32)
    return result.astype(jnp.bfloat16)


def solution(mesh):
    in_specs = (
        P(("row", "col"), None),
        P(),
        P(),
        P("row", "col"),
        P("col"),
        P("col", "row"),
        P(),
        P(),
        P(),
        P("row", "col"),
        P("col"),
        P("row", "col"),
        P(),
    )
    out_specs = P(("row", "col"), None)
    return jax.shard_map(local, mesh=mesh, in_specs=in_specs, out_specs=out_specs, check_vma=False)
```

profile of v0, /device:TPU:0, one launch (start us, length us, event | category | flops | bytes accessed | tf_op | source)
XLA Modules:
  0.0 374.7 jit_solution(7904936646565501967)
XLA Ops:
  6.5 0.0 all-gather.19.cloned.1.call-start
  6.5 0.7 all-gather.19.cloned.1.call-update
  7.3 0.0 all-gather.9.cloned.1.call-start
  7.3 0.7 convert_element_type.64
  8.0 0.7 convert_element_type.65
  8.7 1.3 convert_reduce_fusion.1
  10.0 1.4 fusion.37
  11.4 2.3 fusion.40
  13.7 0.0 all-gather.9.cloned.1.call-update
  13.8 0.0 all-gather.11.cloned.1.call-start
  13.8 25.0 %all-gather.1 = bf16[4,352,176]{1,2,0:T(8,128)(2,1)S(1)} all-gather(bf16[1,352,176]{1,2,0:T(8,128)(2,1)} %bitcast.70), channel_id=1, replica_groups=mesh['row'=4,'col'=8] {'row'}, dimensions={0}, use_global_device_ids=true | all-gather | bytes 619520 | tf_op jit(solution)/shard_map/all_gather | solution.py:65
  38.8 0.2 copy.31
  39.0 1.2 reshape.54
  40.2 0.0 all-gather.11.cloned.1.call-update
  40.2 0.0 all-gather.15.cloned.1.call-start
  40.3 0.5 all-gather.15.cloned.1.call-update
  40.8 0.0 all-gather.17.cloned.1.call-start
  40.8 0.5 all-gather.17.cloned.1.call-update
  41.4 0.0 copy-done.6
  41.4 14.3 %all-gather.19.cloned.1.call-done = bf16[4,352,528]{1,2,0:T(8,128)(2,1)} async-done(((bf16[1,352,528]{1,2,0:T(8,128)(2,1)}), bf16[4,352,528]{1,2,0:T(8,128)(2,1)}) %all-gather.19.cloned.1.call-update) | async-done | bytes 1486864 | tf_op jit(solution)/shard_map/all_gather | solution.py:64
  55.7 2.0 copy.24
  57.8 1.2 reshape.52
  58.9 41.5 %all-gather.9.cloned.1.call-done = bf16[2048,1408]{1,0:T(8,128)(2,1)} async-done(((bf16[256,1408]{1,0:T(8,128)(2,1)}), bf16[2048,1408]{1,0:T(8,128)(2,1)}) %all-gather.9.cloned.1.call-update) | async-done | bytes 5767184 | tf_op jit(solution)/shard_map/all_gather | solution.py:73
  100.5 6.4 %add_convert_fusion = bf16[2048,528]{0,1:T(8,128)(2,1)S(1)} fusion(bf16[2048,1408]{1,0:T(8,128)(2,1)} %all-gather.9.cloned.1.call-done, bf16[1408,528]{0,1:T(8,128)(2,1)S(1)} %reshape.52, f32[528]{0:T(1024)S(1)} %convert_element_type.67), kind=kOutput, calls=%fused_computation.40 | convolution fusion | flops 3047227392 | bytes 9418816 | tf_op jit(solution)/shard_map/dot_general | solution.py:72
  106.9 0.0 copy-start.1
  106.9 1.1 slice_bitcast_fusion
  108.0 0.5 reshape_squeeze.3
  108.6 0.1 copy.28
  108.7 0.0 copy-start.2
  108.7 0.0 copy-start.3
  108.7 0.0 copy-start.4
  108.7 48.0 %while.10 = (s32[]{:T(128)}, bf16[4,512,176]{1,2,0:T(8,128)(2,1)S(1)}, bf16[4,512,2,88]{1,3,2,0:T(8,128)(2,1)S(1)}, bf16[2048,2,88]{0,2,1:T(8,128)(2,1)}, bf16[2048,2,88]{0,2,1:T(8,128)(2,1)S(1)}, /*index=5*/s32[]{:T(128)}) while((s32[]{:T(128)}, bf16[4,512,176]{1,2,0:T(8,128)(2,1)S(1)}, bf16[4,512,2,88]{1,3,2,0:T(8,128)(2,1)S(1)}, ...), condition=%wide.region_5.6_spmd, body=%wide.region_2.5_spmd.sunk | while | flops 748775424 | bytes 18948172 | solution.py:37
  108.7 7.1 %fusion.96 = (f32[2,512]{1,0:T(2,128)S(1)}, f32[2,512,2048]{2,1,0:T(8,128)}) fusion(bf16[2048,2,88]{0,2,1:T(8,128)(2,1)} %get-tuple-element.108, bf16[4,512,2,88]{1,3,2,0:T(8,128)(2,1)S(1)} %get-tuple-element.107, s32[]{:T(128)} %get-tuple-element.99), kind=kOutput, calls=%fused_computation.93.clone.1 | convolution fusion | flops 375392256 | bytes 9293828 | tf_op jit(solution)/shard_map/while/body/eval_jaxpr/sub | solution.py:32
  115.9 4.9 %fusion.97 = bf16[2,512,88]{1,2,0:T(8,128)(2,1)S(1)} fusion(bf16[2048,2,88]{0,2,1:T(8,128)(2,1)S(1)} %get-tuple-element.109, f32[2,512,2048]{2,1,0:T(8,128)} %get-tuple-element.91, f32[2,512]{1,0:T(2,128)S(1)} %get-tuple-element.92), kind=kOutput, calls=%fused_computation.7.clone.1 | convolution fusion | flops 373383168 | bytes 9293824 | tf_op jit(solution)/shard_map/while/body/eval_jaxpr/hqk,khe->qhe/dot_general | solution.py:34
  120.8 7.0 %fusion.96 = (f32[2,512]{1,0:T(2,128)S(1)}, f32[2,512,2048]{2,1,0:T(8,128)}) fusion(bf16[2048,2,88]{0,2,1:T(8,128)(2,1)} %get-tuple-element.108, bf16[4,512,2,88]{1,3,2,0:T(8,128)(2,1)S(1)} %get-tuple-element.107, s32[]{:T(128)} %get-tuple-element.99), kind=kOutput, calls=%fused_computation.93.clone.1 | convolution fusion | flops 375392256 | bytes 9293828 | tf_op jit(solution)/shard_map/while/body/eval_jaxpr/sub | solution.py:32
  127.8 4.9 %fusion.97 = bf16[2,512,88]{1,2,0:T(8,128)(2,1)S(1)} fusion(bf16[2048,2,88]{0,2,1:T(8,128)(2,1)S(1)} %get-tuple-element.109, f32[2,512,2048]{2,1,0:T(8,128)} %get-tuple-element.91, f32[2,512]{1,0:T(2,128)S(1)} %get-tuple-element.92), kind=kOutput, calls=%fused_computation.7.clone.1 | convolution fusion | flops 373383168 | bytes 9293824 | tf_op jit(solution)/shard_map/while/body/eval_jaxpr/hqk,khe->qhe/dot_general | solution.py:34
  132.8 7.0 %fusion.96 = (f32[2,512]{1,0:T(2,128)S(1)}, f32[2,512,2048]{2,1,0:T(8,128)}) fusion(bf16[2048,2,88]{0,2,1:T(8,128)(2,1)} %get-tuple-element.108, bf16[4,512,2,88]{1,3,2,0:T(8,128)(2,1)S(1)} %get-tuple-element.107, s32[]{:T(128)} %get-tuple-element.99), kind=kOutput, calls=%fused_computation.93.clone.1 | convolution fusion | flops 375392256 | bytes 9293828 | tf_op jit(solution)/shard_map/while/body/eval_jaxpr/sub | solution.py:32
  139.8 4.9 %fusion.97 = bf16[2,512,88]{1,2,0:T(8,128)(2,1)S(1)} fusion(bf16[2048,2,88]{0,2,1:T(8,128)(2,1)S(1)} %get-tuple-element.109, f32[2,512,2048]{2,1,0:T(8,128)} %get-tuple-element.91, f32[2,512]{1,0:T(2,128)S(1)} %get-tuple-element.92), kind=kOutput, calls=%fused_computation.7.clone.1 | convolution fusion | flops 373383168 | bytes 9293824 | tf_op jit(solution)/shard_map/while/body/eval_jaxpr/hqk,khe->qhe/dot_general | solution.py:34
  144.7 7.1 %fusion.96 = (f32[2,512]{1,0:T(2,128)S(1)}, f32[2,512,2048]{2,1,0:T(8,128)}) fusion(bf16[2048,2,88]{0,2,1:T(8,128)(2,1)} %get-tuple-element.108, bf16[4,512,2,88]{1,3,2,0:T(8,128)(2,1)S(1)} %get-tuple-element.107, s32[]{:T(128)} %get-tuple-element.99), kind=kOutput, calls=%fused_computation.93.clone.1 | convolution fusion | flops 375392256 | bytes 9293828 | tf_op jit(solution)/shard_map/while/body/eval_jaxpr/sub | solution.py:32
  151.8 4.9 %fusion.97 = bf16[2,512,88]{1,2,0:T(8,128)(2,1)S(1)} fusion(bf16[2048,2,88]{0,2,1:T(8,128)(2,1)S(1)} %get-tuple-element.109, f32[2,512,2048]{2,1,0:T(8,128)} %get-tuple-element.91, f32[2,512]{1,0:T(2,128)S(1)} %get-tuple-element.92), kind=kOutput, calls=%fused_computation.7.clone.1 | convolution fusion | flops 373383168 | bytes 9293824 | tf_op jit(solution)/shard_map/while/body/eval_jaxpr/hqk,khe->qhe/dot_general | solution.py:34
  156.7 0.6 copy.29
  157.3 0.2 all_to_all.12
  157.4 1.0 copy.30
  158.4 3.5 all-to-all-start
  162.0 0.2 all-gather.13.cloned.1.call-start
  162.3 0.0 copy-done.4
  162.3 0.0 all-gather.11.cloned.1.call-done
  162.3 11.4 %all-to-all-done = bf16[8,256,176]{1,2,0:T(8,128)(2,1)S(1)} async-done(((bf16[8,256,176]{1,2,0:T(8,128)(2,1)}), bf16[8,256,176]{1,2,0:T(8,128)(2,1)S(1)}, u32[]{:S(2)}, u32[]{:S(2)}) %all-to-all-start) | async-done | bytes 720928 | tf_op jit(solution)/shard_map/all_to_all | solution.py:84
  173.7 4.0 %convolution_convert_fusion.1 = bf16[8,256,1408]{2,1,0:T(8,128)(2,1)S(1)} fusion(bf16[8,176,1408]{2,1,0:T(8,128)(2,1)} %bitcast.66, bf16[8,256,176]{1,2,0:T(8,128)(2,1)S(1)} %all-to-all-done), kind=kOutput, calls=%fused_computation.39 | convolution fusion | flops 1017905152 | bytes 10452992 | tf_op jit(solution)/shard_map/rgc,gcd->grd/dot_general | solution.py:87
  177.8 0.0 copy-start.7
  177.8 0.8 convert_reduce_fusion
  178.6 0.3 fusion.73
  178.9 0.4 multiply_reduce_fusion.1
  179.3 1.3 add_convert_fusion.2
  180.6 0.0 all-gather.13.cloned.1.call-update
  180.6 0.0 reduce-scatter.2.cloned.1.call-start
  180.7 0.0 copy-start.5
  180.7 5.5 %all-gather.15.cloned.1.call-done = bf16[1408,768]{1,0:T(8,128)(2,1)} async-done(((bf16[352,768]{1,0:T(8,128)(2,1)}), bf16[1408,768]{1,0:T(8,128)(2,1)}) %all-gather.15.cloned.1.call-update) | async-done | bytes 2162704 | tf_op jit(solution)/shard_map/all_gather | solution.py:66
  186.2 47.0 %all-gather.17.cloned.1.call-done = bf16[1408,768]{1,0:T(8,128)(2,1)} async-done(((bf16[352,768]{1,0:T(8,128)(2,1)}), bf16[1408,768]{1,0:T(8,128)(2,1)}) %all-gather.17.cloned.1.call-update) | async-done | bytes 2162704 | tf_op jit(solution)/shard_map/all_gather | solution.py:67
  233.2 43.7 %all-gather.13.cloned.1.call-done = bf16[2048,1408]{1,0:T(8,128)(2,1)} async-done(((bf16[256,1408]{1,0:T(8,128)(2,1)}), bf16[2048,1408]{1,0:T(8,128)(2,1)}) %all-gather.13.cloned.1.call-update) | async-done | bytes 5767184 | tf_op jit(solution)/shard_map/all_gather | solution.py:94
  276.9 29.4 %convolution_convert_fusion = bf16[2048,1408]{1,0:T(8,128)(2,1)} fusion(bf16[1408,768]{1,0:T(8,128)(2,1)} %all-gather.17.cloned.1.call-done, bf16[2048,1408]{1,0:T(8,128)(2,1)} %all-gather.13.cloned.1.call-done, bf16[1408,768]{1,0:T(8,128)(2,1)} %all-gather.15.cloned.1.call-done, f32[768]{0:T(1024)S(1)} %convert_element_type.75), kind=kOutput, calls=%fused_computation.20 | convolution fusion | flops 8965062656 | bytes 15862784 | tf_op jit(solution)/shard_map/dot_general | solution.py:41
  306.4 0.0 reduce-scatter.2.cloned.1.call-update
  306.4 59.1 %reduce-scatter.2.cloned.1.call-done = bf16[256,1408]{1,0:T(8,128)(2,1)} async-done(((bf16[2048,1408]{1,0:T(8,128)(2,1)}), bf16[256,1408]{1,0:T(8,128)(2,1)}) %reduce-scatter.2.cloned.1.call-update) | async-done | bytes 720912 | tf_op jit(solution)/shard_map/reduce_scatter | solution.py:101
  365.5 2.3 add_convert_fusion.1
  (23 shorter events, 0.1 us)
Async XLA Ops:
  6.5 34.8 %copy-start.6 = (bf16[528]{0:T(1024)(128)(2,1)S(1)}, bf16[528]{0:T(1024)(128)(2,1)}, u32[]{:S(2)}) copy-start(bf16[528]{0:T(1024)(128)(2,1)} %param.19) | copy-start | bytes 3172
  6.5 49.2 %all-gather.19.cloned.1.call-start = ((), (), s32[]{:S(2)}) async-start(), calls=%async_computation.8 | async-start | bytes 2027520 | tf_op jit(solution)/shard_map/all_gather | solution.py:64
  7.3 93.2 %all-gather.9.cloned.1.call-start = ((), (), s32[]{:S(2)}) async-start(), calls=%async_computation.2 | async-start | bytes 6488064 | tf_op jit(solution)/shard_map/all_gather | solution.py:73
  13.8 148.5 %all-gather.11.cloned.1.call-start = ((), (), s32[]{:S(2)}) async-start(), calls=%async_computation.3 | async-start | bytes 4460544 | tf_op jit(solution)/shard_map/all_gather | solution.py:81
  40.2 146.0 %all-gather.15.cloned.1.call-start = ((), (), s32[]{:S(2)}) async-start(), calls=%async_computation.5 | async-start | bytes 2703360 | tf_op jit(solution)/shard_map/all_gather | solution.py:66
  40.8 192.4 %all-gather.17.cloned.1.call-start = ((), (), s32[]{:S(2)}) async-start(), calls=%async_computation.6 | async-start | bytes 2703360 | tf_op jit(solution)/shard_map/all_gather | solution.py:67
  106.9 1.8 copy-start.1
  108.7 53.5 %copy-start.2 = (bf16[1408]{0:T(1024)(128)(2,1)S(1)}, bf16[1408]{0:T(1024)(128)(2,1)}, u32[]{:S(2)}) copy-start(bf16[1408]{0:T(1024)(128)(2,1)} %param.21) | copy-start | bytes 8452
  108.7 53.5 %copy-start.3 = (bf16[1408]{0:T(1024)(128)(2,1)S(1)}, bf16[1408]{0:T(1024)(128)(2,1)}, u32[]{:S(2)}) copy-start(bf16[1408]{0:T(1024)(128)(2,1)} %param.22) | copy-start | bytes 8452
  108.7 53.5 %copy-start.4 = (bf16[1408]{0:T(1024)(128)(2,1)S(1)}, bf16[1408]{0:T(1024)(128)(2,1)}, u32[]{:S(2)}) copy-start(bf16[1408]{0:T(1024)(128)(2,1)} %param.23) | copy-start | bytes 8452
  158.4 15.3 %all-to-all-start = ((bf16[8,256,176]{1,2,0:T(8,128)(2,1)}), bf16[8,256,176]{1,2,0:T(8,128)(2,1)S(1)}, u32[]{:S(2)}, u32[]{:S(2)}) async-start(bf16[8,256,176]{1,2,0:T(8,128)(2,1)} %copy.30), calls=%async_computation | async-start | bytes 1441792 | tf_op jit(solution)/shard_map/all_to_all | solution.py:84
  162.0 114.9 %all-gather.13.cloned.1.call-start = ((), (), s32[]{:S(2)}) async-start(), calls=%async_computation.4 | async-start | bytes 6488064 | tf_op jit(solution)/shard_map/all_gather | solution.py:94
  173.7 4.9 %copy-start = (bf16[256,1408]{1,0:T(8,128)(2,1)S(1)}, bf16[256,1408]{1,0:T(8,128)(2,1)}, u32[]{:S(2)}) copy-start(bf16[256,1408]{1,0:T(8,128)(2,1)} %param.15) | copy-start | bytes 2162692
  177.8 2.9 copy-start.7
  180.6 184.9 %reduce-scatter.2.cloned.1.call-start = ((), (), s32[]{:S(2)}) async-start(), calls=%async_computation.7 | async-start | bytes 6488064 | tf_op jit(solution)/shard_map/reduce_scatter | solution.py:101
  180.7 125.7 %copy-start.5 = (bf16[1408]{0:T(1024)(128)(2,1)S(1)}, bf16[1408]{0:T(1024)(128)(2,1)}, u32[]{:S(2)}) copy-start(bf16[1408]{0:T(1024)(128)(2,1)} %param.27) | copy-start | bytes 8452
Sparse Core Ops, SparseCore 0:
  8.9 46.7 all-gather.18
  57.6 42.8 all-gather.8
  102.4 35.6 all-gather.10
  139.4 46.7 all-gather.14
  187.6 45.5 all-gather.16
  234.9 41.9 all-gather.12
  306.5 58.9 reduce-scatter.1
where the time goes:
time: 375 us
  waiting for transfers between devices  225 us (60%)
  matrix products  87.7 us (23%)
  blocking collectives  25 us (7%)
  between operations  13.8 us (4%)
  other arithmetic  11.5 us (3%)
  local copies, waits for them, and re-layouts  8.19 us (2%)
  starting transfers between devices  3.97 us (1%)
    reduce_scatter x1, waiting for transfers between devices, local(): lax.psum_scatter(project_back(hidden, fc2_full).astype(jnp.bfloat16), 'co...  59.1 us
    all_gather x1, waiting for transfers between devices, local(): fc2_full = lax.all_gather(fc2_weight, 'row', axis=0, tiled=True)  47 us
    all_gather x1, waiting for transfers between devices, local(): lax.all_gather(ln2, 'col', axis=0, tiled=True)  43.7 us
    all_gather x1, waiting for transfers between devices, local(): lax.all_gather(ln1, 'col', axis=0, tiled=True)  41.5 us
    dot_general x1, matrix products, project_back(): lax.dot_general(left, right, (((1,), (1,)), ((), ())), preferred_element_...  29.4 us
    sub x4, matrix products, one_block(): expo = jnp.exp(scores - top)  28.3 us
    all_gather x1, blocking collectives, local(): proj_full = lax.all_gather(proj_weight, 'row', axis=1, tiled=True)  25 us
    dot_general x4, matrix products, one_block(): jnp.einsum('hqk,khe->qhe', probs, values, preferred_element_type=jnp.floa...  19.5 us
  transfers between devices with their start and end apart: 8, of which 7 were waited for; matrix products, arithmetic and copies ran while one was open for 20% of the time, Pallas kernels for 0%

commit v1 on v0

--- a/solution.py
+++ b/solution.py
@@ -62,7 +62,7 @@
     own_rows = tokens_in.shape[0]
     inputs = tokens_in.astype(jnp.float32)
     qkv_full = lax.all_gather(qkv_weight, "row", axis=0, tiled=True)
-    proj_full = lax.all_gather(proj_weight, "row", axis=1, tiled=True)
+    proj_full = jnp.concatenate(lax.all_gather(proj_weight, "row"), axis=1)
     fc1_full = lax.all_gather(fc1_weight, "row", axis=0, tiled=True)
     fc2_full = lax.all_gather(fc2_weight, "row", axis=0, tiled=True)
     qkv_shift = qkv_bias.astype(jnp.float32)

time: 375 us -> 375 us (level)
  no operation moved by 1% of the time
where the time goes in v1:
time: 375 us
  waiting for transfers between devices  225 us (60%)
  matrix products  87.7 us (23%)
  blocking collectives  25 us (7%)
  between operations  13.8 us (4%)
  other arithmetic  11.5 us (3%)
  local copies, waits for them, and re-layouts  8.19 us (2%)
  starting transfers between devices  3.97 us (1%)
    reduce_scatter x1, waiting for transfers between devices, local(): lax.psum_scatter(project_back(hidden, fc2_full).astype(jnp.bfloat16), 'co...  59.1 us
    all_gather x1, waiting for transfers between devices, local(): fc2_full = lax.all_gather(fc2_weight, 'row', axis=0, tiled=True)  47 us
    all_gather x1, waiting for transfers between devices, local(): lax.all_gather(ln2, 'col', axis=0, tiled=True)  43.7 us
    all_gather x1, waiting for transfers between devices, local(): lax.all_gather(ln1, 'col', axis=0, tiled=True)  41.5 us
    dot_general x1, matrix products, project_back(): lax.dot_general(left, right, (((1,), (1,)), ((), ())), preferred_element_...  29.4 us
    sub x4, matrix products, one_block(): expo = jnp.exp(scores - top)  28.3 us
    all_gather x1, blocking collectives, local(): proj_full = jnp.concatenate(lax.all_gather(proj_weight, 'row'), axis=1)  25 us
    dot_general x4, matrix products, one_block(): jnp.einsum('hqk,khe->qhe', probs, values, preferred_element_type=jnp.floa...  19.5 us
  transfers between devices with their start and end apart: 8, of which 7 were waited for; matrix products, arithmetic and copies ran while one was open for 20% of the time, Pallas kernels for 0%

profile of v1, /device:TPU:0, one launch (start us, length us, event | category | flops | bytes accessed | tf_op | source)
XLA Modules:
  0.0 374.7 jit_solution(9084854517247199095)
XLA Ops:
  6.5 0.0 all-gather.19.cloned.1.call-start
  6.5 0.7 all-gather.19.cloned.1.call-update
  7.3 0.0 all-gather.9.cloned.1.call-start
  7.3 0.7 convert_element_type.64
  8.0 0.7 convert_element_type.65
  8.7 1.3 convert_reduce_fusion.1
  10.0 1.4 fusion.37
  11.4 2.3 fusion.40
  13.7 0.0 all-gather.9.cloned.1.call-update
  13.8 0.0 all-gather.11.cloned.1.call-start
  13.8 25.0 %all-gather = bf16[704,352]{1,0:T(8,128)(2,1)S(1)} all-gather(bf16[176,352]{1,0:T(8,128)(2,1)} %param.20), channel_id=2, replica_groups=mesh['row'=4,'col'=8] {'row'}, dimensions={0}, use_global_device_ids=true | all-gather | bytes 619520 | tf_op jit(solution)/shard_map/all_gather | solution.py:65
  38.8 0.2 copy.32
  39.0 1.2 reshape.57
  40.2 0.0 all-gather.11.cloned.1.call-update
  40.2 0.0 all-gather.15.cloned.1.call-start
  40.3 0.5 all-gather.15.cloned.1.call-update
  40.8 0.0 all-gather.17.cloned.1.call-start
  40.8 0.5 all-gather.17.cloned.1.call-update
  41.4 14.3 %all-gather.19.cloned.1.call-done = bf16[4,352,528]{1,2,0:T(8,128)(2,1)} async-done(((bf16[1,352,528]{1,2,0:T(8,128)(2,1)}), bf16[4,352,528]{1,2,0:T(8,128)(2,1)}) %all-gather.19.cloned.1.call-update) | async-done | bytes 1486864 | tf_op jit(solution)/shard_map/all_gather | solution.py:64
  55.7 2.0 copy.25
  57.8 1.2 reshape.61
  58.9 41.5 %all-gather.9.cloned.1.call-done = bf16[2048,1408]{1,0:T(8,128)(2,1)} async-done(((bf16[256,1408]{1,0:T(8,128)(2,1)}), bf16[2048,1408]{1,0:T(8,128)(2,1)}) %all-gather.9.cloned.1.call-update) | async-done | bytes 5767184 | tf_op jit(solution)/shard_map/all_gather | solution.py:73
  100.5 6.4 %add_convert_fusion = bf16[2048,528]{0,1:T(8,128)(2,1)S(1)} fusion(bf16[2048,1408]{1,0:T(8,128)(2,1)} %all-gather.9.cloned.1.call-done, bf16[1408,528]{0,1:T(8,128)(2,1)S(1)} %reshape.61, f32[528]{0:T(1024)S(1)} %convert_element_type.67), kind=kOutput, calls=%fused_computation.40 | convolution fusion | flops 3047227392 | bytes 9418816 | tf_op jit(solution)/shard_map/dot_general | solution.py:72
  106.9 0.0 copy-start.1
  106.9 1.1 slice_bitcast_fusion
  108.0 0.5 reshape_squeeze.3
  108.6 0.1 copy.29
  108.7 0.0 copy-start.2
  108.7 0.0 copy-start.3
  108.7 0.0 copy-start.4
  108.7 48.0 %while.10 = (s32[]{:T(128)}, bf16[4,512,176]{1,2,0:T(8,128)(2,1)S(1)}, bf16[4,512,2,88]{1,3,2,0:T(8,128)(2,1)S(1)}, bf16[2048,2,88]{0,2,1:T(8,128)(2,1)}, bf16[2048,2,88]{0,2,1:T(8,128)(2,1)S(1)}, /*index=5*/s32[]{:T(128)}) while((s32[]{:T(128)}, bf16[4,512,176]{1,2,0:T(8,128)(2,1)S(1)}, bf16[4,512,2,88]{1,3,2,0:T(8,128)(2,1)S(1)}, ...), condition=%wide.region_5.6_spmd, body=%wide.region_2.5_spmd.sunk | while | flops 748775424 | bytes 18948172 | solution.py:37
  108.7 7.1 %fusion.96 = (f32[2,512]{1,0:T(2,128)S(1)}, f32[2,512,2048]{2,1,0:T(8,128)}) fusion(bf16[2048,2,88]{0,2,1:T(8,128)(2,1)} %get-tuple-element.108, bf16[4,512,2,88]{1,3,2,0:T(8,128)(2,1)S(1)} %get-tuple-element.107, s32[]{:T(128)} %get-tuple-element.99), kind=kOutput, calls=%fused_computation.93.clone.1 | convolution fusion | flops 375392256 | bytes 9293828 | tf_op jit(solution)/shard_map/while/body/eval_jaxpr/sub | solution.py:32
  115.9 4.9 %fusion.97 = bf16[2,512,88]{1,2,0:T(8,128)(2,1)S(1)} fusion(bf16[2048,2,88]{0,2,1:T(8,128)(2,1)S(1)} %get-tuple-element.109, f32[2,512,2048]{2,1,0:T(8,128)} %get-tuple-element.91, f32[2,512]{1,0:T(2,128)S(1)} %get-tuple-element.92), kind=kOutput, calls=%fused_computation.7.clone.1 | convolution fusion | flops 373383168 | bytes 9293824 | tf_op jit(solution)/shard_map/while/body/eval_jaxpr/hqk,khe->qhe/dot_general | solution.py:34
  120.8 7.0 %fusion.96 = (f32[2,512]{1,0:T(2,128)S(1)}, f32[2,512,2048]{2,1,0:T(8,128)}) fusion(bf16[2048,2,88]{0,2,1:T(8,128)(2,1)} %get-tuple-element.108, bf16[4,512,2,88]{1,3,2,0:T(8,128)(2,1)S(1)} %get-tuple-element.107, s32[]{:T(128)} %get-tuple-element.99), kind=kOutput, calls=%fused_computation.93.clone.1 | convolution fusion | flops 375392256 | bytes 9293828 | tf_op jit(solution)/shard_map/while/body/eval_jaxpr/sub | solution.py:32
  127.8 4.9 %fusion.97 = bf16[2,512,88]{1,2,0:T(8,128)(2,1)S(1)} fusion(bf16[2048,2,88]{0,2,1:T(8,128)(2,1)S(1)} %get-tuple-element.109, f32[2,512,2048]{2,1,0:T(8,128)} %get-tuple-element.91, f32[2,512]{1,0:T(2,128)S(1)} %get-tuple-element.92), kind=kOutput, calls=%fused_computation.7.clone.1 | convolution fusion | flops 373383168 | bytes 9293824 | tf_op jit(solution)/shard_map/while/body/eval_jaxpr/hqk,khe->qhe/dot_general | solution.py:34
  132.8 7.0 %fusion.96 = (f32[2,512]{1,0:T(2,128)S(1)}, f32[2,512,2048]{2,1,0:T(8,128)}) fusion(bf16[2048,2,88]{0,2,1:T(8,128)(2,1)} %get-tuple-element.108, bf16[4,512,2,88]{1,3,2,0:T(8,128)(2,1)S(1)} %get-tuple-element.107, s32[]{:T(128)} %get-tuple-element.99), kind=kOutput, calls=%fused_computation.93.clone.1 | convolution fusion | flops 375392256 | bytes 9293828 | tf_op jit(solution)/shard_map/while/body/eval_jaxpr/sub | solution.py:32
  139.8 4.9 %fusion.97 = bf16[2,512,88]{1,2,0:T(8,128)(2,1)S(1)} fusion(bf16[2048,2,88]{0,2,1:T(8,128)(2,1)S(1)} %get-tuple-element.109, f32[2,512,2048]{2,1,0:T(8,128)} %get-tuple-element.91, f32[2,512]{1,0:T(2,128)S(1)} %get-tuple-element.92), kind=kOutput, calls=%fused_computation.7.clone.1 | convolution fusion | flops 373383168 | bytes 9293824 | tf_op jit(solution)/shard_map/while/body/eval_jaxpr/hqk,khe->qhe/dot_general | solution.py:34
  144.7 7.1 %fusion.96 = (f32[2,512]{1,0:T(2,128)S(1)}, f32[2,512,2048]{2,1,0:T(8,128)}) fusion(bf16[2048,2,88]{0,2,1:T(8,128)(2,1)} %get-tuple-element.108, bf16[4,512,2,88]{1,3,2,0:T(8,128)(2,1)S(1)} %get-tuple-element.107, s32[]{:T(128)} %get-tuple-element.99), kind=kOutput, calls=%fused_computation.93.clone.1 | convolution fusion | flops 375392256 | bytes 9293828 | tf_op jit(solution)/shard_map/while/body/eval_jaxpr/sub | solution.py:32
  151.8 4.9 %fusion.97 = bf16[2,512,88]{1,2,0:T(8,128)(2,1)S(1)} fusion(bf16[2048,2,88]{0,2,1:T(8,128)(2,1)S(1)} %get-tuple-element.109, f32[2,512,2048]{2,1,0:T(8,128)} %get-tuple-element.91, f32[2,512]{1,0:T(2,128)S(1)} %get-tuple-element.92), kind=kOutput, calls=%fused_computation.7.clone.1 | convolution fusion | flops 373383168 | bytes 9293824 | tf_op jit(solution)/shard_map/while/body/eval_jaxpr/hqk,khe->qhe/dot_general | solution.py:34
  156.7 0.6 copy.30
  157.3 0.2 all_to_all.12
  157.4 1.0 copy.31
  158.4 3.5 all-to-all-start
  162.0 0.2 all-gather.13.cloned.1.call-start
  162.3 0.0 copy-done.4
  162.3 0.0 all-gather.11.cloned.1.call-done
  162.3 11.4 %all-to-all-done = bf16[8,256,176]{1,2,0:T(8,128)(2,1)S(1)} async-done(((bf16[8,256,176]{1,2,0:T(8,128)(2,1)}), bf16[8,256,176]{1,2,0:T(8,128)(2,1)S(1)}, u32[]{:S(2)}, u32[]{:S(2)}) %all-to-all-start) | async-done | bytes 720928 | tf_op jit(solution)/shard_map/all_to_all | solution.py:84
  173.7 4.0 %convolution_convert_fusion.1 = bf16[8,256,1408]{2,1,0:T(8,128)(2,1)S(1)} fusion(bf16[8,176,1408]{2,1,0:T(8,128)(2,1)} %bitcast.63, bf16[8,256,176]{1,2,0:T(8,128)(2,1)S(1)} %all-to-all-done), kind=kOutput, calls=%fused_computation.39 | convolution fusion | flops 1017905152 | bytes 10452992 | tf_op jit(solution)/shard_map/rgc,gcd->grd/dot_general | solution.py:87
  177.8 0.0 copy-start.7
  177.8 0.8 convert_reduce_fusion
  178.6 0.3 fusion.73
  178.9 0.4 multiply_reduce_fusion.1
  179.3 1.3 add_convert_fusion.2
  180.6 0.0 all-gather.13.cloned.1.call-update
  180.6 0.0 reduce-scatter.2.cloned.1.call-start
  180.6 0.0 copy-done.7
  180.7 0.0 copy-start.5
  180.7 5.5 %all-gather.15.cloned.1.call-done = bf16[1408,768]{1,0:T(8,128)(2,1)} async-done(((bf16[352,768]{1,0:T(8,128)(2,1)}), bf16[1408,768]{1,0:T(8,128)(2,1)}) %all-gather.15.cloned.1.call-update) | async-done | bytes 2162704 | tf_op jit(solution)/shard_map/all_gather | solution.py:66
  186.2 47.0 %all-gather.17.cloned.1.call-done = bf16[1408,768]{1,0:T(8,128)(2,1)} async-done(((bf16[352,768]{1,0:T(8,128)(2,1)}), bf16[1408,768]{1,0:T(8,128)(2,1)}) %all-gather.17.cloned.1.call-update) | async-done | bytes 2162704 | tf_op jit(solution)/shard_map/all_gather | solution.py:67
  233.2 43.7 %all-gather.13.cloned.1.call-done = bf16[2048,1408]{1,0:T(8,128)(2,1)} async-done(((bf16[256,1408]{1,0:T(8,128)(2,1)}), bf16[2048,1408]{1,0:T(8,128)(2,1)}) %all-gather.13.cloned.1.call-update) | async-done | bytes 5767184 | tf_op jit(solution)/shard_map/all_gather | solution.py:94
  276.9 29.4 %convolution_convert_fusion = bf16[2048,1408]{1,0:T(8,128)(2,1)} fusion(bf16[1408,768]{1,0:T(8,128)(2,1)} %all-gather.17.cloned.1.call-done, bf16[2048,1408]{1,0:T(8,128)(2,1)} %all-gather.13.cloned.1.call-done, bf16[1408,768]{1,0:T(8,128)(2,1)} %all-gather.15.cloned.1.call-done, f32[768]{0:T(1024)S(1)} %convert_element_type.75), kind=kOutput, calls=%fused_computation.20 | convolution fusion | flops 8965062656 | bytes 15862784 | tf_op jit(solution)/shard_map/dot_general | solution.py:41
  306.4 0.0 reduce-scatter.2.cloned.1.call-update
  306.4 59.1 %reduce-scatter.2.cloned.1.call-done = bf16[256,1408]{1,0:T(8,128)(2,1)} async-done(((bf16[2048,1408]{1,0:T(8,128)(2,1)}), bf16[256,1408]{1,0:T(8,128)(2,1)}) %reduce-scatter.2.cloned.1.call-update) | async-done | bytes 720912 | tf_op jit(solution)/shard_map/reduce_scatter | solution.py:101
  365.5 2.3 add_convert_fusion.1
  (23 shorter events, 0.1 us)
Async XLA Ops:
  6.5 34.8 %copy-start.6 = (bf16[528]{0:T(1024)(128)(2,1)S(1)}, bf16[528]{0:T(1024)(128)(2,1)}, u32[]{:S(2)}) copy-start(bf16[528]{0:T(1024)(128)(2,1)} %param.19) | copy-start | bytes 3172
  6.5 49.2 %all-gather.19.cloned.1.call-start = ((), (), s32[]{:S(2)}) async-start(), calls=%async_computation.8 | async-start | bytes 2027520 | tf_op jit(solution)/shard_map/all_gather | solution.py:64
  7.3 93.2 %all-gather.9.cloned.1.call-start = ((), (), s32[]{:S(2)}) async-start(), calls=%async_computation.2 | async-start | bytes 6488064 | tf_op jit(solution)/shard_map/all_gather | solution.py:73
  13.8 148.5 %all-gather.11.cloned.1.call-start = ((), (), s32[]{:S(2)}) async-start(), calls=%async_computation.3 | async-start | bytes 4460544 | tf_op jit(solution)/shard_map/all_gather | solution.py:81
  40.2 146.0 %all-gather.15.cloned.1.call-start = ((), (), s32[]{:S(2)}) async-start(), calls=%async_computation.5 | async-start | bytes 2703360 | tf_op jit(solution)/shard_map/all_gather | solution.py:66
  40.8 192.4 %all-gather.17.cloned.1.call-start = ((), (), s32[]{:S(2)}) async-start(), calls=%async_computation.6 | async-start | bytes 2703360 | tf_op jit(solution)/shard_map/all_gather | solution.py:67
  106.9 1.8 copy-start.1
  108.7 53.5 %copy-start.2 = (bf16[1408]{0:T(1024)(128)(2,1)S(1)}, bf16[1408]{0:T(1024)(128)(2,1)}, u32[]{:S(2)}) copy-start(bf16[1408]{0:T(1024)(128)(2,1)} %param.21) | copy-start | bytes 8452
  108.7 53.5 %copy-start.3 = (bf16[1408]{0:T(1024)(128)(2,1)S(1)}, bf16[1408]{0:T(1024)(128)(2,1)}, u32[]{:S(2)}) copy-start(bf16[1408]{0:T(1024)(128)(2,1)} %param.22) | copy-start | bytes 8452
  108.7 53.5 %copy-start.4 = (bf16[1408]{0:T(1024)(128)(2,1)S(1)}, bf16[1408]{0:T(1024)(128)(2,1)}, u32[]{:S(2)}) copy-start(bf16[1408]{0:T(1024)(128)(2,1)} %param.23) | copy-start | bytes 8452
  158.4 15.3 %all-to-all-start = ((bf16[8,256,176]{1,2,0:T(8,128)(2,1)}), bf16[8,256,176]{1,2,0:T(8,128)(2,1)S(1)}, u32[]{:S(2)}, u32[]{:S(2)}) async-start(bf16[8,256,176]{1,2,0:T(8,128)(2,1)} %copy.31), calls=%async_computation | async-start | bytes 1441792 | tf_op jit(solution)/shard_map/all_to_all | solution.py:84
  162.0 114.9 %all-gather.13.cloned.1.call-start = ((), (), s32[]{:S(2)}) async-start(), calls=%async_computation.4 | async-start | bytes 6488064 | tf_op jit(solution)/shard_map/all_gather | solution.py:94
  173.7 4.9 %copy-start = (bf16[256,1408]{1,0:T(8,128)(2,1)S(1)}, bf16[256,1408]{1,0:T(8,128)(2,1)}, u32[]{:S(2)}) copy-start(bf16[256,1408]{1,0:T(8,128)(2,1)} %param.15) | copy-start | bytes 2162692
  177.8 2.9 copy-start.7
  180.6 184.9 %reduce-scatter.2.cloned.1.call-start = ((), (), s32[]{:S(2)}) async-start(), calls=%async_computation.7 | async-start | bytes 6488064 | tf_op jit(solution)/shard_map/reduce_scatter | solution.py:101
  180.7 125.7 %copy-start.5 = (bf16[1408]{0:T(1024)(128)(2,1)S(1)}, bf16[1408]{0:T(1024)(128)(2,1)}, u32[]{:S(2)}) copy-start(bf16[1408]{0:T(1024)(128)(2,1)} %param.27) | copy-start | bytes 8452
Sparse Core Ops, SparseCore 0:
  8.9 46.7 all-gather.18
  57.6 42.8 all-gather.8
  102.4 35.6 all-gather.10
  139.4 46.7 all-gather.14
  187.6 45.5 all-gather.16
  234.9 41.9 all-gather.12
  306.5 58.9 reduce-scatter.1
